TPU v7x, 32 devices: a whole 2x2x4 slice. The times are simulated.
32 devices in a mesh: groups: 2 (over x), pb: 16 (over z, y, core).
Axes of the slice: x: 2, y: 2, z: 4, core: 2. Of those that a mesh axis runs over, the one named last changes fastest.
Arguments:
- tokens: bfloat16 [6144, 512], P(('groups', 'pb')), parts along dimension 0, may hold values from -6 to 6
- stamps: int32 [6144], P(('groups', 'pb')), parts along dimension 0, may hold values from 0 to 1086324736, as said below
- norm_gain: float32 [512], replicated, may hold values from 0.5 to 1.5
- w_proj: bfloat16 [512, 2048], replicated, may hold values from -0.25 to 0.25
- rel_bias: float32 [8, 16], replicated, may hold values from -1.5 to 1.5
- attn_gain: float32 [512], replicated, may hold values from 0.5 to 1.5
- w_out: bfloat16 [512, 512], replicated, may hold values from -0.25 to 0.25
Outputs:
- mixed: bfloat16 [6144, 512], P(('groups', 'pb')), parts along dimension 0
There are 2 independent parts, one for each index of `groups`. A program takes and returns all parts, laid end to end along the dimension named above; an argument that names none is the same for every part. Nothing has to cross between parts.
Inputs may be any that keep to these rules, and one draw needn't show every extreme that they name: `stamps`: stamps never fall from one row to the next.
All inputs are finite; a program needn't handle non-finite values.
Results may differ from a plain program's by a relative error of at most 0.008.
Values may be sent and summed in bfloat16 or wider, within the bound.
A program may use at most 128 MiB of HBM per device.

v0:
```python
import jax
import jax.numpy as jnp
from jax import lax
from jax.sharding import PartitionSpec as P

HEADS = 8
BUCKETS = 16


epsilon = 1e-05


def layer_norm(values, gain):
    centered = values - jnp.mean(values, axis=-1, keepdims=True)
    spread = jnp.mean(centered * centered, axis=-1, keepdims=True)
    return centered * lax.rsqrt(spread + epsilon) * gain


def bucket_of(elapsed):
    bucket_ids = jnp.zeros(elapsed.shape, jnp.int32)
    for exponent in range(BUCKETS - 1):
        bucket_ids = bucket_ids + (elapsed >= 4**exponent).astype(jnp.int32)
    return bucket_ids


def relative_bias(bias_table, bucket):
    bias = jnp.zeros((bias_table.shape[0],) + bucket.shape, jnp.float32)
    for bucket_id in range(BUCKETS):
        bias = jnp.where((bucket == bucket_id)[None], bias_table[:, bucket_id][:, None, None], bias)
    return bias


def attend(queries, key_rows, value_rows, query_pos, key_pos, query_stamp, key_stamp, bias_table):
    query_count = queries.shape[0]
    key_count = key_rows.shape[0]
    head_size = queries.shape[1] // HEADS
    q_heads = queries.reshape(query_count, HEADS, head_size)
    k_heads = key_rows.reshape(key_count, HEADS, head_size)
    v_heads = value_rows.reshape(key_count, HEADS, head_size)
    scores = jnp.einsum(
        "qhd,khd->hqk", q_heads, k_heads, preferred_element_type=jnp.float32
    ) * head_size ** (-0.5)
    bucket = bucket_of(query_stamp[:, None] - key_stamp[None, :])
    scores = scores + relative_bias(bias_table, bucket)
    visible = key_pos[None, :] <= query_pos[:, None]
    weight = jnp.where(visible[None], jax.nn.silu(scores), 0.0).astype(jnp.bfloat16)
    mixture = jnp.einsum("hqk,khd->qhd", weight, v_heads, preferred_element_type=jnp.float32)
    return mixture.reshape(query_count, HEADS * head_size)


def body(tokens, stamps, norm_gain, w_proj, rel_bias, attn_gain, w_out):
    my_index = lax.axis_index("pb")
    row_count, tok_width = tokens.shape
    every_stamp = lax.all_gather(stamps, "pb", axis=0, tiled=True)
    row_index = jnp.arange(row_count, dtype=jnp.int32)
    own_pos = my_index * row_count + row_index
    own_stamp = jnp.take(every_stamp, own_pos)
    normed = layer_norm(tokens.astype(jnp.float32), norm_gain).astype(jnp.bfloat16)
    front_proj = jnp.dot(normed, w_proj[:, : 2 * tok_width], preferred_element_type=jnp.float32)
    gate_vals = jax.nn.silu(front_proj[:, :tok_width]).astype(jnp.bfloat16)
    queries = front_proj[:, tok_width:].astype(jnp.bfloat16)
    back_weight = w_proj[:, 2 * tok_width :]

    def visit_block(running, key_block, value_block, first_row):
        key_count = key_block.shape[0]
        key_pos = first_row + jnp.arange(key_count, dtype=jnp.int32)
        key_stamp = lax.dynamic_slice_in_dim(every_stamp, first_row, key_count, 0)
        return lax.cond(
            first_row <= my_index * row_count + row_count - 1,
            lambda: running
            + attend(
                queries, key_block, value_block, own_pos, key_pos, own_stamp, key_stamp, rel_bias
            ),
            lambda: running,
        )

    def from_inputs(partial_sum, blocks, first_row):
        both_proj = jnp.dot(blocks[0], back_weight, preferred_element_type=jnp.float32)
        key_block = both_proj[:, :tok_width].astype(jnp.bfloat16)
        value_block = both_proj[:, tok_width:].astype(jnp.bfloat16)
        return visit_block(partial_sum, key_block, value_block, first_row)

    empty_sum = jnp.zeros((row_count, tok_width), jnp.float32)
    piece = (lax.all_gather(normed, "pb", axis=0, tiled=True),)
    shard_count = piece[0].shape[0] // row_count
    group_size = 1
    for candidate in range(1, shard_count + 1):
        if shard_count % candidate == 0 and candidate * row_count <= 2048:
            group_size = candidate
    block_length = group_size * row_count

    def one_group(group_step, partial_sum):
        blocks = tuple(
            (
                lax.dynamic_slice_in_dim(member, group_step * block_length, block_length, 0)
                for member in piece
            )
        )
        return from_inputs(partial_sum, blocks, group_step * block_length)

    attended = lax.fori_loop(0, shard_count // group_size, one_group, empty_sum)
    gated = (layer_norm(attended, attn_gain) * gate_vals.astype(jnp.float32)).astype(jnp.bfloat16)
    result = (
        tokens.astype(jnp.float32) + jnp.dot(gated, w_out, preferred_element_type=jnp.float32)
    ).astype(jnp.bfloat16)
    return result


def solution(mesh):
    return jax.shard_map(
        body,
        mesh=mesh,
        in_specs=(P(("groups", "pb"), None), P(("groups", "pb")), P(), P(), P(), P(), P()),
        out_specs=P(("groups", "pb"), None),
        check_vma=False,
    )
```

profile of v0, /device:TPU:29, one launch (start us, length us, event | category | flops | bytes accessed | tf_op | source)
XLA Modules:
  0.0 168.3 jit_solution(9190498993229262674)
XLA Ops:
  6.5 0.0 copy-start
  6.5 0.0 copy-start.1
  6.5 0.0 all-gather.2.cloned.1.call-start
  6.5 1.2 convert_reduce_fusion
  7.7 1.1 fusion.13
  8.9 1.8 %fusion.15 = bf16[192,512]{1,0:T(8,128)(2,1)} fusion(bf16[192,512]{1,0:T(8,128)(2,1)} %param.11, f32[512]{0:T(512)} %param.13, f32[192]{0:T(256)S(1)} %add_rsqrt_fusion.1, f32[192]{0:T(256)S(1)} %broadcast_multiply_fusion.1), kind=kLoop, calls=%fused_computation.72 | loop fusion | flops 491520 | bytes 396800 | tf_op jit(solution)/shard_map/convert_element_type | solution.py:58
  10.6 0.0 copy-start.2
  10.7 0.0 all-gather.2.cloned.1.call-update
  10.7 0.8 copy.16
  11.5 0.0 copy-start.6
  11.5 0.0 copy-start.4
  11.5 2.3 %slice.81 = bf16[512,1024]{1,0:T(8,128)(2,1)} slice(bf16[512,2048]{1,0:T(8,128)(2,1)} %param.14), slice={[0:512], [1024:2048]} | slice | bytes 2097152 | tf_op jit(solution)/shard_map/slice | solution.py:62
  13.8 0.0 copy-done.1
  13.8 0.0 copy-done.2
  13.8 0.4 fusion.9
  14.2 0.0 copy-start.3
  14.2 0.9 copy-done.3
  15.1 0.8 copy.15
  15.9 0.0 copy-done.6
  16.0 0.6 dynamic-slice
  17.1 0.0 copy-done.4
  17.1 0.3 dynamic-update-slice
  17.4 57.4 %all-reduce = s32[3072]{0:T(1024)S(1)} all-reduce(s32[3072]{0:T(1024)S(1)} %dynamic-update-slice), channel_id=1, replica_groups=mesh['groups'=2,'pb'=16] {'pb'}, use_global_device_ids=true, to_apply=%add | all-reduce | flops 3072 | bytes 24576
  74.8 1.4 gather_fusion
  76.2 0.0 all-gather.2.cloned.1.call-done
  76.3 0.0 copy-start.5
  76.3 82.6 %while.19 = (s32[]{:T(128)}, f32[192,512]{0,1:T(8,128)S(1)}, s32[]{:T(128)}, bf16[3072,512]{1,0:T(8,128)(2,1)}, bf16[512,1024]{1,0:T(8,128)(2,1)}, /*index=5*/bf...) while((s32[]{:T(128)}, f32[192,512]{0,1:T(8,128)S(1)}, ...), condition=%wide.region_5.6_spmd.clone, body=%wide.region_2.0_spmd.clone.sunk | while | flops 2291173120 | bytes 41205836 | solution.py:101
  76.4 5.2 %convolution_convert_fusion.2 = bf16[1536,1024]{1,0:T(8,128)(2,1)} fusion(bf16[512,1024]{1,0:T(8,128)(2,1)} %get-tuple-element.503, bf16[3072,512]{1,0:T(8,128)(2,1)} %get-tuple-element.502, s32[]{:T(128)} %select_n.144), kind=kOutput, calls=%fused_computation.59.clone.1 | convolution fusion | flops 1612185600 | bytes 5767680 | tf_op jit(solution)/shard_map/while/body/eval_jaxpr/dot_general | solution.py:78
  81.5 36.1 %conditional.3 = (f32[192,512]{0,1:T(8,128)S(1)}) conditional(s32[]{:T(128)} %convert_element_type.1355, f32[192,512]{0,1:T(8,128)S(1)} %get-tuple-element.486, (s32[]{:T(128)}, s32[1536]{0:T(1024)S(1)}, s32[]{:T(128)}, bf16[192,512]{0,1:T(8,128)(2,1)}, bf16[1536,1024]{1,0:T(8,128)(2,1)}, /*index=5*/s32[192]{0:T(256)S(1)}, s32[3072]{0:T(1024)S(1)}, ...), branch_computations={%region_3.3_spmd, %region_4.4_spmd} | conditional | flops 678987456 | bytes 35430956 | solution.py:68
  81.5 0.1 dynamic_slice.16
  81.6 0.2 broadcast_compare_fusion.16
  81.9 4.7 %copy.14 = bf16[1536,1024]{0,1:T(8,128)(2,1)} copy(bf16[1536,1024]{1,0:T(8,128)(2,1)} %get-tuple-element.343) | data formatting | bytes 6291456 | tf_op jit(solution)/shard_map
  86.6 4.7 %copy.13 = bf16[1536,1024]{0,1:T(8,128)(2,1)} copy(bf16[1536,1024]{1,0:T(8,128)(2,1)} %get-tuple-element.343) | data formatting | bytes 6291456 | tf_op jit(solution)/shard_map
  91.3 2.7 %slice.89 = bf16[1536,512]{0,1:T(8,128)(2,1)} slice(bf16[1536,1024]{0,1:T(8,128)(2,1)} %copy.13), slice={[0:1536], [0:512]} | slice | bytes 3145728 | tf_op jit(solution)/shard_map/while/body/eval_jaxpr/slice | solution.py:79
  94.0 0.0 slice-start
  94.0 5.7 %broadcast_compare_fusion.13 = (pred[192,1536]{1,0:T(8,128)(4,1)}, pred[192,1536]{1,0:T(8,128)(4,1)}, pred[192,1536]{1,0:T(8,128)(4,1)}, pred[192,1536]{1,0:T(8,...) fusion(s32[1536]{0:T(1024)S(1)} %dynamic_slice.16, ...), kind=kLoop, calls=%fused_computation.33 | loop fusion | flops 17989632 | bytes 4725504 | tf_op jit(solution)/shard_map/while/body/eval_jaxpr/cond/branch_1_fun/eq | solution.py:29
  99.7 0.0 slice-done
  99.7 17.8 %fusion.2 = f32[8,192,64]{1,2,0:T(8,128)S(1)} fusion(bf16[1536,8,64]{0,2,1:T(8,128)(2,1)S(1)} %bitcast.49, bf16[192,8,64]{0,2,1:T(8,128)(2,1)} %bitcast, bf16[1536,8,64]{0,2,1:T(8,128)(2,1)} %bitcast.50, f32[8]{0:T(128)S(1)} %get-tuple-element.409, f32[8]{0:T(128)S(1)} %get-tuple-element.395, f32[8]{0:T(128)S(1)} %get-tuple-element.396, ...), kind=kOutput, calls=%fused_computation.18 | convolution fusion | flops 660602880 | bytes 8749568 | tf_op jit(solution)/shard_map/while/body/eval_jaxpr/cond/branch_1_fun/hqk,khd->qhd/dot_general | solution.py:47
  117.5 0.1 bitcast_add_fusion
  117.7 5.2 %convolution_convert_fusion.2 = bf16[1536,1024]{1,0:T(8,128)(2,1)} fusion(bf16[512,1024]{1,0:T(8,128)(2,1)} %get-tuple-element.503, bf16[3072,512]{1,0:T(8,128)(2,1)} %get-tuple-element.502, s32[]{:T(128)} %select_n.144), kind=kOutput, calls=%fused_computation.59.clone.1 | convolution fusion | flops 1612185600 | bytes 5767680 | tf_op jit(solution)/shard_map/while/body/eval_jaxpr/dot_general | solution.py:78
  122.8 36.1 %conditional.3 = (f32[192,512]{0,1:T(8,128)S(1)}) conditional(s32[]{:T(128)} %convert_element_type.1355, f32[192,512]{0,1:T(8,128)S(1)} %get-tuple-element.486, (s32[]{:T(128)}, s32[1536]{0:T(1024)S(1)}, s32[]{:T(128)}, bf16[192,512]{0,1:T(8,128)(2,1)}, bf16[1536,1024]{1,0:T(8,128)(2,1)}, /*index=5*/s32[192]{0:T(256)S(1)}, s32[3072]{0:T(1024)S(1)}, ...), branch_computations={%region_3.3_spmd, %region_4.4_spmd} | conditional | flops 678987456 | bytes 35430956 | solution.py:68
  122.8 0.1 dynamic_slice.16
  122.9 0.2 broadcast_compare_fusion.16
  123.2 4.7 %copy.14 = bf16[1536,1024]{0,1:T(8,128)(2,1)} copy(bf16[1536,1024]{1,0:T(8,128)(2,1)} %get-tuple-element.343) | data formatting | bytes 6291456 | tf_op jit(solution)/shard_map
  127.9 4.7 %copy.13 = bf16[1536,1024]{0,1:T(8,128)(2,1)} copy(bf16[1536,1024]{1,0:T(8,128)(2,1)} %get-tuple-element.343) | data formatting | bytes 6291456 | tf_op jit(solution)/shard_map
  132.5 2.7 %slice.89 = bf16[1536,512]{0,1:T(8,128)(2,1)} slice(bf16[1536,1024]{0,1:T(8,128)(2,1)} %copy.13), slice={[0:1536], [0:512]} | slice | bytes 3145728 | tf_op jit(solution)/shard_map/while/body/eval_jaxpr/slice | solution.py:79
  135.3 0.0 slice-start
  135.3 5.7 %broadcast_compare_fusion.13 = (pred[192,1536]{1,0:T(8,128)(4,1)}, pred[192,1536]{1,0:T(8,128)(4,1)}, pred[192,1536]{1,0:T(8,128)(4,1)}, pred[192,1536]{1,0:T(8,...) fusion(s32[1536]{0:T(1024)S(1)} %dynamic_slice.16, ...), kind=kLoop, calls=%fused_computation.33 | loop fusion | flops 17989632 | bytes 4725504 | tf_op jit(solution)/shard_map/while/body/eval_jaxpr/cond/branch_1_fun/eq | solution.py:29
  141.0 0.0 slice-done
  141.0 17.8 %fusion.2 = f32[8,192,64]{1,2,0:T(8,128)S(1)} fusion(bf16[1536,8,64]{0,2,1:T(8,128)(2,1)S(1)} %bitcast.49, bf16[192,8,64]{0,2,1:T(8,128)(2,1)} %bitcast, bf16[1536,8,64]{0,2,1:T(8,128)(2,1)} %bitcast.50, f32[8]{0:T(128)S(1)} %get-tuple-element.409, f32[8]{0:T(128)S(1)} %get-tuple-element.395, f32[8]{0:T(128)S(1)} %get-tuple-element.396, ...), kind=kOutput, calls=%fused_computation.18 | convolution fusion | flops 660602880 | bytes 8749568 | tf_op jit(solution)/shard_map/while/body/eval_jaxpr/cond/branch_1_fun/hqk,khd->qhd/dot_general | solution.py:47
  158.8 0.1 bitcast_add_fusion
  158.9 0.1 reduce_sum.38
  159.0 0.2 copy.17
  159.2 0.2 multiply_reduce_fusion
  159.4 0.0 copy-done
  159.4 0.0 copy-done.5
  159.4 2.1 %fusion.8 = bf16[192,512]{1,0:T(8,128)(2,1)} fusion(bf16[512,512]{1,0:T(8,128)(2,1)S(1)} %copy-done, bf16[192,512]{1,0:T(8,128)(2,1)} %param.11, f32[192,512]{1,0:T(8,128)S(1)} %copy.17, f32[192,1024]{1,0:T(8,128)} %copy-done.3, f32[512]{0:T(512)S(1)} %copy-done.5, f32[192]{0:T(256)S(1)} %add_rsqrt_fusion, f32[192]{0:T(256)S(1)} %broadcast_multiply_fusion), kind=kOutput, calls=%fused_computation.63 | convolution fusion | flops 102039552 | bytes 1707520 | tf_op jit(solution)/shard_map/dot_general | solution.py:104
  (20 shorter events, 0.1 us)
Async XLA Ops:
  6.5 152.9 %copy-start = (bf16[512,512]{1,0:T(8,128)(2,1)S(1)}, bf16[512,512]{1,0:T(8,128)(2,1)}, u32[]{:S(2)}) copy-start(bf16[512,512]{1,0:T(8,128)(2,1)} %param.17) | copy-start | bytes 1572868
  6.5 7.3 %copy-start.1 = (bf16[512,2048]{1,0:T(8,128)(2,1)S(1)}, bf16[512,2048]{1,0:T(8,128)(2,1)}, u32[]{:S(2)}) copy-start(bf16[512,2048]{1,0:T(8,128)(2,1)} %param.14) | copy-start | bytes 6291460
  6.5 69.7 %all-gather.2.cloned.1.call-start = ((), (), s32[]{:S(2)}) async-start(), calls=%async_computation | async-start | bytes 3342336 | tf_op jit(solution)/shard_map/all_gather | solution.py:84
  10.6 3.1 %copy-start.2 = (bf16[192,512]{1,0:T(8,128)(2,1)S(1)}, bf16[192,512]{1,0:T(8,128)(2,1)}, u32[]{:S(2)}) copy-start(bf16[192,512]{1,0:T(8,128)(2,1)} %fusion.15) | copy-start | bytes 589828
  11.5 4.5 %copy-start.6 = (u32[32]{0:T(128)S(1)}, u32[32]{0:T(128)}, u32[]{:S(2)}) copy-start(u32[32]{0:T(128)} %constant.154) | copy-start | bytes 388
  11.5 5.6 %copy-start.4 = (s32[192]{0:T(256)S(1)}, s32[192]{0:T(256)}, u32[]{:S(2)}) copy-start(s32[192]{0:T(256)} %param.12) | copy-start | bytes 2308
  14.2 0.9 copy-start.3
  76.3 83.1 %copy-start.5 = (f32[512]{0:T(512)S(1)}, f32[512]{0:T(512)}, u32[]{:S(2)}) copy-start(f32[512]{0:T(512)} %param.16) | copy-start | bytes 6148
  94.0 5.7 %slice-start = ((bf16[1536,1024]{0,1:T(8,128)(2,1)}), bf16[1536,512]{0,1:T(8,128)(2,1)S(1)}, s32[]{:S(2)}) async-start(bf16[1536,1024]{0,1:T(8,128)(2,1)} %copy.14), calls=%async_computation.1 | async-start | bytes 3145728 | tf_op jit(solution)/shard_map/while/body/eval_jaxpr/slice | solution.py:80
  135.3 5.7 %slice-start = ((bf16[1536,1024]{0,1:T(8,128)(2,1)}), bf16[1536,512]{0,1:T(8,128)(2,1)S(1)}, s32[]{:S(2)}) async-start(bf16[1536,1024]{0,1:T(8,128)(2,1)} %copy.14), calls=%async_computation.1 | async-start | bytes 3145728 | tf_op jit(solution)/shard_map/while/body/eval_jaxpr/slice | solution.py:80
Sparse Core Ops, SparseCore 0:
  10.8 44.4 all-gather.1
where the time goes:
time: 169 us; the launch traced here: 168 us
  blocking collectives  57.4 us (34%)
  matrix products  48.4 us (29%)
  local copies, waits for them, and re-layouts  31.8 us (19%)
  other arithmetic  16.5 us (10%)
  between operations  14.1 us (8%)
    unnamed x1, blocking collectives  57.4 us
    dot_general x2, matrix products, attend(): jnp.einsum('hqk,khd->qhd', weight, v_heads, preferred_element_type=jnp.fl...  35.6 us
    another operation x4, local copies, waits for them, and re-layouts  18.8 us
    eq x2, other arithmetic, relative_bias(): bucket == bucket_id  11.4 us
    dot_general x2, matrix products, from_inputs(): jnp.dot(blocks[0], back_weight, preferred_element_type=jnp.float32)  10.3 us
    slice x2, local copies, waits for them, and re-layouts, from_inputs(): key_block = both_proj[:, :tok_width].astype(jnp.bfloat16)  5.41 us
    unnamed x19, local copies, waits for them, and re-layouts  3.41 us
  transfers between devices with their start and end apart: 1, of which 0 were waited for; matrix products, arithmetic and copies ran while one was open for 4% of the time, Pallas kernels for 0%

commit v1 on v0

v1 whole, which is shorter than its diff:
```python
import functools

import jax
import jax.numpy as jnp
from jax import lax
from jax.experimental import pallas as pl
from jax.experimental.pallas import tpu as pltpu
from jax.sharding import PartitionSpec as P

EPSILON = 1e-05
LANES = 128


def layer_norm(values, gain):
    centered = values - jnp.mean(values, axis=-1, keepdims=True)
    spread = jnp.mean(centered * centered, axis=-1, keepdims=True)
    return centered * lax.rsqrt(spread + EPSILON) * gain


def kernel(
    parts,
    heads,
    tokens_ref,
    stamps_ref,
    norm_gain_ref,
    w_proj_ref,
    bias_ref,
    attn_gain_ref,
    w_out_ref,
    out_ref,
    send_buf,
    kvq,
    stamp_all,
    stamp_keys,
    gate_buf,
    back_buf,
    att_buf,
    send_sem,
    fwd_sem,
    kv_sem,
    stamp_send_sem,
    stamp_sem,
    back_sem,
    att_sem,
):
    rows, width = tokens_ref.shape
    half = rows // 2
    head_size = width // heads
    splits = parts // heads
    slots = parts // splits
    blocks_per_tile = max(1, 384 // rows)
    key_tile = blocks_per_tile * rows
    buckets = bias_ref.shape[1]

    me = lax.axis_index("pb")
    my_head = me // splits
    my_split = me % splits

    def split_of(block):
        place = block % splits
        odd = (block // splits) % 2
        return place + odd * (splits - 1 - 2 * place)

    def block_of(slot, split):
        odd = slot % 2
        return slot * splits + split + odd * (splits - 1 - 2 * split)

    barrier = pltpu.get_barrier_semaphore()

    def greet(step, carry):
        other = lax.rem(me + step, parts)
        pl.semaphore_signal(
            barrier, inc=1, device_id={"pb": other}, device_id_type=pl.DeviceIdType.MESH
        )
        return carry

    lax.fori_loop(1, parts, greet, 0)

    low = lax.broadcasted_iota(jnp.int32, (1, LANES), 1) < head_size

    normed = layer_norm(tokens_ref[...].astype(jnp.float32), norm_gain_ref[...]).astype(jnp.bfloat16)
    front = jnp.dot(normed, w_proj_ref[:, width : 2 * width], preferred_element_type=jnp.float32)
    scaled = front.astype(jnp.bfloat16).astype(jnp.float32) * (0.5 * head_size ** (-0.5))
    back = jnp.dot(normed, w_proj_ref[:, 2 * width :], preferred_element_type=jnp.float32)
    for pair in range(heads // 2):
        cols = slice(pair * LANES, (pair + 1) * LANES)
        key_cols = back[:, :width][:, cols]
        value_cols = back[:, width:][:, cols]
        query_cols = scaled[:, cols]
        send_buf[2 * pair, :rows, :] = jnp.where(
            low, key_cols, pltpu.roll(value_cols, head_size, 1)
        ).astype(jnp.bfloat16)
        send_buf[2 * pair + 1, :rows, :] = jnp.where(
            low, pltpu.roll(key_cols, head_size, 1), value_cols
        ).astype(jnp.bfloat16)
        top, bottom = query_cols[:half], query_cols[half:]
        send_buf[2 * pair, rows:, :] = jnp.where(
            low, top, pltpu.roll(bottom, head_size, 1)
        ).astype(jnp.bfloat16)
        send_buf[2 * pair + 1, rows:, :] = jnp.where(
            low, pltpu.roll(top, head_size, 1), bottom
        ).astype(jnp.bfloat16)
    gate_proj = jnp.dot(normed, w_proj_ref[:, :width], preferred_element_type=jnp.float32)
    gate_buf[...] = jax.nn.silu(gate_proj).astype(jnp.bfloat16)

    pl.semaphore_wait(barrier, parts - 1)

    my_home = split_of(me)

    def payload(head, target):
        return pltpu.make_async_remote_copy(
            src_ref=send_buf.at[head],
            dst_ref=kvq.at[me],
            send_sem=send_sem.at[head],
            recv_sem=kv_sem.at[me],
            device_id={"pb": target},
            device_id_type=pl.DeviceIdType.MESH,
        )

    def each_payload(act):
        def one(step, carry):
            head = lax.rem(my_head + step, heads)
            target = head * splits + my_home

            @pl.when(target != me)
            def _():
                act(payload(head, target))

            return carry

        lax.fori_loop(0, heads, one, 0)

    def stamp_copy(target):
        return pltpu.make_async_remote_copy(
            src_ref=stamps_ref,
            dst_ref=stamp_all.at[me],
            send_sem=stamp_send_sem.at[target],
            recv_sem=stamp_sem.at[me],
            device_id={"pb": target},
            device_id_type=pl.DeviceIdType.MESH,
        )

    def stamp_arrival(source):
        return pltpu.make_async_remote_copy(
            src_ref=stamps_ref,
            dst_ref=stamp_all.at[source],
            send_sem=stamp_send_sem.at[source],
            recv_sem=stamp_sem.at[source],
            device_id={"pb": source},
            device_id_type=pl.DeviceIdType.MESH,
        )

    each_payload(lambda copy: copy.start())

    def send_stamps(step, carry):
        stamp_copy(lax.rem(me + step, parts)).start()
        return carry

    lax.fori_loop(1, parts, send_stamps, 0)

    stamp_all[me] = stamps_ref[...]

    @pl.when(my_home == my_split)
    def _():
        kvq[me] = send_buf[my_head]

    zeros_count = lax.broadcasted_iota(jnp.int32, (8, LANES), 1)
    bucket = jnp.clip((33 - zeros_count) >> 1, 0, buckets - 1)
    table = jnp.zeros((8, LANES), jnp.float32)
    for bucket_id in range(buckets):
        table = jnp.where(bucket == bucket_id, 0.5 * bias_ref[my_head, bucket_id], table)
    table = jnp.broadcast_to(table[:1], (rows, LANES))

    def arrival(source):
        return pltpu.make_async_remote_copy(
            src_ref=send_buf.at[0],
            dst_ref=kvq.at[source],
            send_sem=send_sem.at[0],
            recv_sem=kv_sem.at[source],
            device_id={"pb": source},
            device_id_type=pl.DeviceIdType.MESH,
        )

    def forward(slot, source, step):
        peer = my_head * splits + lax.rem(my_split + step, splits)
        return pltpu.make_async_remote_copy(
            src_ref=kvq.at[source, pl.ds(0, rows)],
            dst_ref=kvq.at[source, pl.ds(0, rows)],
            send_sem=fwd_sem.at[slot, step],
            recv_sem=kv_sem.at[source],
            device_id={"pb": peer},
            device_id_type=pl.DeviceIdType.MESH,
        )

    def take_direct(slot, carry):
        source = block_of(slot, my_split)

        @pl.when(source != me)
        def _():
            arrival(source).wait_recv()

        for step in range(1, splits):
            forward(slot, source, step).start()
        return carry

    lax.fori_loop(0, slots, take_direct, 0)

    def wait_stamps(step, carry):
        stamp_arrival(lax.rem(me + step, parts)).wait_recv()
        return carry

    lax.fori_loop(1, parts, wait_stamps, 0)

    for tile in range(parts // blocks_per_tile):
        stamp_keys[tile] = jnp.concatenate(
            [stamp_all[tile * blocks_per_tile + place] for place in range(blocks_per_tile)], axis=1
        )

    def send_back(slot, target):
        return pltpu.make_async_remote_copy(
            src_ref=back_buf.at[slot],
            dst_ref=att_buf.at[my_head],
            send_sem=back_sem.at[slot],
            recv_sem=att_sem.at[my_head],
            device_id={"pb": target},
            device_id_type=pl.DeviceIdType.MESH,
        )

    row_id = lax.broadcasted_iota(jnp.int32, (rows, LANES), 0)
    col_id = lax.broadcasted_iota(jnp.int32, (rows, LANES), 1)

    def one_slot(slot, carry):
        block = block_of(slot, my_split)
        for step in range(1, splits):
            source = block_of(slot, lax.rem(my_split + step, splits))
            forward(slot, source, step).wait_recv()
        packed = kvq[block, rows:, :].astype(jnp.float32)
        queries = jnp.concatenate(
            [jnp.where(low, packed, 0.0), jnp.where(low, pltpu.roll(packed, head_size, 1), 0.0)], axis=0
        ).astype(jnp.bfloat16)
        query_stamp = jnp.transpose(jnp.broadcast_to(stamp_all[block], (LANES, rows)))

        def visit(tile, total, masked):
            key_value = kvq[pl.ds(tile * blocks_per_tile, blocks_per_tile), :rows, :]
            key_value = key_value.reshape(key_tile, LANES)
            scores = lax.dot_general(
                queries, key_value, (((1,), (1,)), ((), ())), preferred_element_type=jnp.float32
            )
            weights = []
            for first in range(0, key_tile, LANES):
                elapsed = query_stamp - stamp_keys[tile, :, first : first + LANES]
                bias = jnp.take_along_axis(table, lax.clz(elapsed), axis=1, mode="promise_in_bounds")
                halved = scores[:, first : first + LANES] + bias
                weight = halved + halved * jnp.tanh(halved)
                if masked:
                    ahead = tile * key_tile + first - block * rows
                    weight = jnp.where(col_id + ahead <= row_id, weight, 0.0)
                weights.append(weight.astype(jnp.bfloat16))
            return total + jnp.dot(
                jnp.concatenate(weights, axis=1), key_value, preferred_element_type=jnp.float32
            )

        last = block // blocks_per_tile
        total = lax.fori_loop(
            0, last, lambda tile, total: visit(tile, total, False), jnp.zeros((rows, LANES), jnp.float32)
        )
        total = visit(last, total, True)
        result = jnp.where(low, pltpu.roll(total[:half], head_size, 1), total[half:]).astype(jnp.bfloat16)
        back_buf[slot] = result

        @pl.when(block == me)
        def _():
            att_buf[my_head] = result

        @pl.when(block != me)
        def _():
            send_back(slot, block).start()

        return carry

    lax.fori_loop(0, slots, one_slot, 0)

    each_payload(lambda copy: copy.wait_send())

    def drain(step, carry):
        stamp_copy(lax.rem(me + step, parts)).wait_send()
        return carry

    lax.fori_loop(1, parts, drain, 0)

    def drain_slot(slot, carry):
        source = block_of(slot, my_split)
        for step in range(1, splits):
            forward(slot, source, step).wait_send()

        @pl.when(source != me)
        def _():
            send_back(slot, source).wait_send()

        return carry

    lax.fori_loop(0, slots, drain_slot, 0)

    def take_back(step, carry):
        head = lax.rem(my_head + step, heads)
        source = head * splits + my_home

        @pl.when(source != me)
        def _():
            pltpu.make_async_remote_copy(
                src_ref=back_buf.at[0],
                dst_ref=att_buf.at[head],
                send_sem=back_sem.at[0],
                recv_sem=att_sem.at[head],
                device_id={"pb": source},
                device_id_type=pl.DeviceIdType.MESH,
            ).wait_recv()

        return carry

    lax.fori_loop(0, heads, take_back, 0)

    pieces = []
    for pair in range(heads // 2):
        even = att_buf[2 * pair].astype(jnp.float32)
        odd = att_buf[2 * pair + 1].astype(jnp.float32)
        pieces.append(
            jnp.concatenate(
                [
                    jnp.where(low, even, pltpu.roll(odd, head_size, 1)),
                    jnp.where(low, pltpu.roll(even, head_size, 1), odd),
                ],
                axis=0,
            )
        )
    attended = jnp.concatenate(pieces, axis=1)
    gated = layer_norm(attended, attn_gain_ref[...]) * gate_buf[...].astype(jnp.float32)
    mixed = tokens_ref[...].astype(jnp.float32) + jnp.dot(
        gated.astype(jnp.bfloat16), w_out_ref[...], preferred_element_type=jnp.float32
    )
    out_ref[...] = mixed.astype(jnp.bfloat16)


def solution(mesh):
    parts = mesh.shape["pb"]

    def body(tokens, stamps, norm_gain, w_proj, rel_bias, attn_gain, w_out):
        rows, width = tokens.shape
        heads = rel_bias.shape[0]
        splits = parts // heads
        slots = parts // splits
        blocks_per_tile = max(1, 384 // rows)
        vmem = pl.BlockSpec(memory_space=pltpu.VMEM)
        smem = pl.BlockSpec(memory_space=pltpu.SMEM)
        return pl.pallas_call(
            functools.partial(kernel, parts, heads),
            out_shape=jax.ShapeDtypeStruct((rows, width), jnp.bfloat16),
            in_specs=[vmem, vmem, vmem, vmem, smem, vmem, vmem],
            out_specs=vmem,
            scratch_shapes=[
                pltpu.VMEM((heads, rows + rows // 2, LANES), jnp.bfloat16),
                pltpu.VMEM((parts, rows + rows // 2, LANES), jnp.bfloat16),
                pltpu.VMEM((parts, 1, rows), jnp.int32),
                pltpu.VMEM((parts // blocks_per_tile, 1, blocks_per_tile * rows), jnp.int32),
                pltpu.VMEM((rows, width), jnp.bfloat16),
                pltpu.VMEM((slots, rows // 2, LANES), jnp.bfloat16),
                pltpu.VMEM((heads, rows // 2, LANES), jnp.bfloat16),
                pltpu.SemaphoreType.DMA((heads,)),
                pltpu.SemaphoreType.DMA((slots, splits)),
                pltpu.SemaphoreType.DMA((parts,)),
                pltpu.SemaphoreType.DMA((parts,)),
                pltpu.SemaphoreType.DMA((parts,)),
                pltpu.SemaphoreType.DMA((slots,)),
                pltpu.SemaphoreType.DMA((heads,)),
            ],
            compiler_params=pltpu.CompilerParams(
                collective_id=0, has_side_effects=True, vmem_limit_bytes=48 * 1024 * 1024
            ),
        )(
            tokens,
            stamps.reshape(1, rows),
            norm_gain.reshape(1, width),
            w_proj,
            rel_bias,
            attn_gain.reshape(1, width),
            w_out,
        )

    return jax.shard_map(
        body,
        mesh=mesh,
        in_specs=(P(("groups", "pb"), None), P(("groups", "pb")), P(), P(), P(), P(), P()),
        out_specs=P(("groups", "pb"), None),
        check_vma=False,
    )
```

time: 169 us -> 47.9 us (0.28)
  the two profiles are of different devices: /device:TPU:29 before, /device:TPU:0 now
where the time goes in v1:
time: 47.9 us; the launch traced here: 47.6 us
  Pallas kernels  40.6 us (85%)
  local copies, waits for them, and re-layouts  6.96 us (15%)
    pallas_call x1, Pallas kernels, body(): pl.pallas_call(functools.partial(kernel, parts, heads), out_shape=jax.Sha...  40.6 us
    unnamed x15, local copies, waits for them, and re-layouts  6.96 us

profile of v1, /device:TPU:0, one launch (start us, length us, event | category | flops | bytes accessed | tf_op | source)
XLA Modules:
  0.0 47.6 jit_solution(3126455722644919256)
XLA Ops:
  0.0 0.0 copy-start
  0.0 1.6 %copy-done = bf16[512,2048]{1,0:T(8,128)(2,1)S(1)} copy-done((bf16[512,2048]{1,0:T(8,128)(2,1)S(1)}, bf16[512,2048]{1,0:T(8,128)(2,1)}, u32[]{:S(2)}) %copy-start) | copy-done | bytes 2097176
  1.6 0.0 copy-start.1
  1.6 1.0 %copy-done.1 = bf16[512,512]{1,0:T(8,128)(2,1)S(1)} copy-done((bf16[512,512]{1,0:T(8,128)(2,1)S(1)}, bf16[512,512]{1,0:T(8,128)(2,1)}, u32[]{:S(2)}) %copy-start.1) | copy-done | bytes 524312
  2.6 0.0 copy-start.2
  2.6 0.9 %copy-done.2 = bf16[192,512]{1,0:T(8,128)(2,1)S(1)} copy-done((bf16[192,512]{1,0:T(8,128)(2,1)S(1)}, bf16[192,512]{1,0:T(8,128)(2,1)}, u32[]{:S(2)}) %copy-start.2) | copy-done | bytes 196632
  3.6 0.0 copy-start.3
  3.6 0.7 %copy-done.3 = f32[8,16]{1,0:T(8,128)S(1)} copy-done((f32[8,16]{1,0:T(8,128)S(1)}, f32[8,16]{1,0:T(8,128)}, u32[]{:S(2)}) %copy-start.3) | copy-done | bytes 536
  4.2 0.0 copy-start.4
  4.3 0.7 %copy-done.4 = f32[512]{0:T(512)S(1)} copy-done((f32[512]{0:T(512)S(1)}, f32[512]{0:T(512)}, u32[]{:S(2)}) %copy-start.4) | copy-done | bytes 2072
  4.9 0.0 copy-start.5
  4.9 0.7 %copy-done.5 = f32[512]{0:T(512)S(1)} copy-done((f32[512]{0:T(512)S(1)}, f32[512]{0:T(512)}, u32[]{:S(2)}) %copy-start.5) | copy-done | bytes 2072
  5.6 0.0 copy-start.6
  5.6 0.7 %copy-done.6 = s32[192]{0:T(256)S(1)} copy-done((s32[192]{0:T(256)S(1)}, s32[192]{0:T(256)}, u32[]{:S(2)}) %copy-start.6) | copy-done | bytes 792
  6.3 40.6 %shard_map.73 = bf16[192,512]{1,0:T(8,128)(2,1)S(1)} custom-call(bf16[192,512]{1,0:T(8,128)(2,1)S(1)} %copy-done.2, s32[1,192]{1,0:T(1,128)S(1)} %bitcast.5, f32[1,512]{1,0:T(1,128)S(1)} %bitcast.3, bf16[512,2048]{1,0:T(8,128)(2,1)S(1)} %copy-done, f32[8,16]{1,0:T(8,128)S(1)} %copy-done.3, f32[1,512]{1,0:T(1,128)S(1)} %bitcast.4, bf16[512,512]{1,0:T(8,128)(2,1)S(1)} %copy-done.1), custom_call_target="tpu_custom_call" | custom-call | tf_op jit(solution)/shard_map/pallas_call | solution.py:355
  46.9 0.7 %copy.9 = bf16[192,512]{1,0:T(8,128)(2,1)} copy(bf16[192,512]{1,0:T(8,128)(2,1)S(1)} %shard_map.73) | data formatting | bytes 393216
Async XLA Ops:
  0.0 1.6 %copy-start = (bf16[512,2048]{1,0:T(8,128)(2,1)S(1)}, bf16[512,2048]{1,0:T(8,128)(2,1)}, u32[]{:S(2)}) copy-start(bf16[512,2048]{1,0:T(8,128)(2,1)} %w_proj_ref.1) | copy-start | bytes 6291460
  1.6 1.0 %copy-start.1 = (bf16[512,512]{1,0:T(8,128)(2,1)S(1)}, bf16[512,512]{1,0:T(8,128)(2,1)}, u32[]{:S(2)}) copy-start(bf16[512,512]{1,0:T(8,128)(2,1)} %w_out_ref.1) | copy-start | bytes 1572868
  2.6 0.9 %copy-start.2 = (bf16[192,512]{1,0:T(8,128)(2,1)S(1)}, bf16[192,512]{1,0:T(8,128)(2,1)}, u32[]{:S(2)}) copy-start(bf16[192,512]{1,0:T(8,128)(2,1)} %tokens_ref.1) | copy-start | bytes 589828
  3.6 0.7 %copy-start.3 = (f32[8,16]{1,0:T(8,128)S(1)}, f32[8,16]{1,0:T(8,128)}, u32[]{:S(2)}) copy-start(f32[8,16]{1,0:T(8,128)} %bias_ref.1) | copy-start | bytes 1540
  4.2 0.7 %copy-start.4 = (f32[512]{0:T(512)S(1)}, f32[512]{0:T(512)}, u32[]{:S(2)}) copy-start(f32[512]{0:T(512)} %param.9) | copy-start | bytes 6148
  4.9 0.7 %copy-start.5 = (f32[512]{0:T(512)S(1)}, f32[512]{0:T(512)}, u32[]{:S(2)}) copy-start(f32[512]{0:T(512)} %param.12) | copy-start | bytes 6148
  5.6 0.7 %copy-start.6 = (s32[192]{0:T(256)S(1)}, s32[192]{0:T(256)}, u32[]{:S(2)}) copy-start(s32[192]{0:T(256)} %param.8) | copy-start | bytes 2308

commit v2 on v1

v2 whole, which is shorter than its diff:
```python
import functools

import jax
import jax.numpy as jnp
from jax import lax
from jax.experimental import pallas as pl
from jax.experimental.pallas import tpu as pltpu
from jax.sharding import PartitionSpec as P

EPSILON = 1e-05
LANES = 128


def layer_norm(values, gain):
    centered = values - jnp.mean(values, axis=-1, keepdims=True)
    spread = jnp.mean(centered * centered, axis=-1, keepdims=True)
    return centered * lax.rsqrt(spread + EPSILON) * gain


def kernel(
    parts,
    heads,
    tokens_hbm,
    stamps_hbm,
    norm_gain_hbm,
    w_proj_hbm,
    bias_hbm,
    attn_gain_hbm,
    w_out_hbm,
    out_ref,
    tokens_ref,
    stamps_ref,
    norm_gain_ref,
    w_proj_ref,
    bias_ref,
    attn_gain_ref,
    w_out_ref,
    kv_send,
    q_send,
    kv_all,
    q_all,
    query_buf,
    stamp_all,
    stamp_keys,
    stamp_rows,
    total_buf,
    gate_buf,
    back_buf,
    att_buf,
    load_sem,
    kv_send_sem,
    q_send_sem,
    fwd_sem,
    kv_sem,
    q_sem,
    stamp_send_sem,
    stamp_sem,
    back_sem,
    att_sem,
):
    rows, width = tokens_ref.shape
    half = rows // 2
    head_size = width // heads
    splits = parts // heads
    slots = heads
    near = slots // 2
    blocks_per_tile = max(1, 384 // rows)
    key_tile = blocks_per_tile * rows
    group_tiles = splits // blocks_per_tile
    buckets = bias_ref.shape[1]

    loads = [
        pltpu.make_async_copy(source, target, load_sem.at[index])
        for index, (source, target) in enumerate(
            [
                (tokens_hbm, tokens_ref),
                (norm_gain_hbm, norm_gain_ref),
                (w_proj_hbm.at[:, width:], w_proj_ref.at[:, width:]),
                (stamps_hbm, stamps_ref),
                (bias_hbm, bias_ref),
                (w_proj_hbm.at[:, :width], w_proj_ref.at[:, :width]),
                (attn_gain_hbm, attn_gain_ref),
                (w_out_hbm, w_out_ref),
            ]
        )
    ]
    for load in loads:
        load.start()

    me = lax.axis_index("pb")
    my_head = me // splits
    my_split = me % splits
    upper = my_head // near
    my_place = my_head % near
    near_first = upper * near
    far_first = near - near_first

    def split_of(block):
        place = block % splits
        odd = (block // splits) % 2
        return place + odd * (splits - 1 - 2 * place)

    def block_of(slot, split):
        odd = slot % 2
        return slot * splits + split + odd * (splits - 1 - 2 * split)

    def remote(source, target, send, receive, device):
        return pltpu.make_async_remote_copy(
            src_ref=source,
            dst_ref=target,
            send_sem=send,
            recv_sem=receive,
            device_id={"pb": device},
            device_id_type=pl.DeviceIdType.MESH,
        )

    barrier = pltpu.get_barrier_semaphore()

    def greet(step, carry):
        other = lax.rem(me + step, parts)
        pl.semaphore_signal(
            barrier, inc=1, device_id={"pb": other}, device_id_type=pl.DeviceIdType.MESH
        )
        return carry

    lax.fori_loop(1, parts, greet, 0)

    low = lax.broadcasted_iota(jnp.int32, (1, LANES), 1) < head_size

    for load in loads[:3]:
        load.wait()
    normed = layer_norm(tokens_ref[...].astype(jnp.float32), norm_gain_ref[...]).astype(jnp.bfloat16)
    front = jnp.dot(normed, w_proj_ref[:, width : 2 * width], preferred_element_type=jnp.float32)
    scaled = front.astype(jnp.bfloat16).astype(jnp.float32) * (0.5 * head_size ** (-0.5))
    back = jnp.dot(normed, w_proj_ref[:, 2 * width :], preferred_element_type=jnp.float32)
    for pair in range(heads // 2):
        cols = slice(pair * LANES, (pair + 1) * LANES)
        key_cols = back[:, :width][:, cols]
        value_cols = back[:, width:][:, cols]
        query_cols = scaled[:, cols]
        kv_send[2 * pair] = jnp.where(
            low, key_cols, pltpu.roll(value_cols, head_size, 1)
        ).astype(jnp.bfloat16)
        kv_send[2 * pair + 1] = jnp.where(
            low, pltpu.roll(key_cols, head_size, 1), value_cols
        ).astype(jnp.bfloat16)
        top, bottom = query_cols[:half], query_cols[half:]
        q_send[2 * pair] = jnp.where(low, top, pltpu.roll(bottom, head_size, 1)).astype(jnp.bfloat16)
        q_send[2 * pair + 1] = jnp.where(low, pltpu.roll(top, head_size, 1), bottom).astype(jnp.bfloat16)
    loads[3].wait()
    loads[4].wait()

    my_home = split_of(me)

    def stamp_copy(target):
        return remote(
            stamps_ref, stamp_all.at[me], stamp_send_sem.at[target], stamp_sem.at[me], target
        )

    def kv_copy(head, target):
        return remote(kv_send.at[head], kv_all.at[me], kv_send_sem.at[head], kv_sem.at[me], target)

    def q_copy(head, target):
        return remote(q_send.at[head], q_all.at[my_head], q_send_sem.at[head], q_sem.at[my_head], target)

    def each_head(first, act):
        def one(step, carry):
            head = first + lax.rem(my_place + step, near)
            target = head * splits + my_home

            @pl.when(target != me)
            def _():
                act(head, target)

            return carry

        lax.fori_loop(0, near, one, 0)

    def send_stamps(step, carry):
        stamp_copy(lax.rem(me + step, parts)).start()
        return carry

    def start_both(head, target):
        q_copy(head, target).start()
        kv_copy(head, target).start()

    pl.semaphore_wait(barrier, parts - 1)
    lax.fori_loop(1, parts, send_stamps, 0)
    each_head(near_first, start_both)
    each_head(far_first, lambda head, target: q_copy(head, target).start())
    each_head(far_first, lambda head, target: kv_copy(head, target).start())

    stamp_all[me] = stamps_ref[...]

    @pl.when(my_home == my_split)
    def _():
        kv_all[me] = kv_send[my_head]
        q_all[my_head] = q_send[my_head]

    loads[5].wait()
    gate_proj = jnp.dot(normed, w_proj_ref[:, :width], preferred_element_type=jnp.float32)
    gate_buf[...] = jax.nn.silu(gate_proj).astype(jnp.bfloat16)
    total_buf[...] = jnp.zeros_like(total_buf)

    zeros_count = lax.broadcasted_iota(jnp.int32, (8, LANES), 1)
    bucket = jnp.clip((33 - zeros_count) >> 1, 0, buckets - 1)
    table = jnp.zeros((8, LANES), jnp.float32)
    for bucket_id in range(buckets):
        table = jnp.where(bucket == bucket_id, 0.5 * bias_ref[my_head, bucket_id], table)
    table = jnp.broadcast_to(table[:1], (rows, LANES))

    def wait_stamps(step, carry):
        source = lax.rem(me + step, parts)
        remote(
            stamps_ref, stamp_all.at[source], stamp_send_sem.at[source], stamp_sem.at[source], source
        ).wait_recv()
        return carry

    lax.fori_loop(1, parts, wait_stamps, 0)

    for tile in range(parts // blocks_per_tile):
        stamp_keys[tile] = jnp.concatenate(
            [stamp_all[tile * blocks_per_tile + place] for place in range(blocks_per_tile)], axis=1
        )

    def turn_stamps(slot, carry):
        block = block_of(slot, my_split)
        stamp_rows[slot] = jnp.transpose(jnp.broadcast_to(stamp_all[block], (LANES, rows)))
        return carry

    lax.fori_loop(0, slots, turn_stamps, 0)

    def forward(slot, source, step):
        peer = my_head * splits + lax.rem(my_split + step, splits)
        return remote(
            kv_all.at[source], kv_all.at[source], fwd_sem.at[slot, step], kv_sem.at[source], peer
        )

    def take_direct(slot):
        source = block_of(slot, my_split)

        @pl.when(source != me)
        def _():
            remote(
                kv_send.at[0], kv_all.at[source], kv_send_sem.at[0], kv_sem.at[source], source
            ).wait_recv()

        for step in range(1, splits):
            forward(slot, source, step).start()

    def take_forwarded(slot):
        for step in range(1, splits):
            source = block_of(slot, lax.rem(my_split + step, splits))
            forward(slot, source, step).wait_recv()

    def take_query(slot):
        source = block_of(slot, my_split)

        @pl.when(source != me)
        def _():
            remote(
                q_send.at[0], q_all.at[slot], q_send_sem.at[0], q_sem.at[slot], source
            ).wait_recv()

        packed = q_all[slot].astype(jnp.float32)
        query_buf[slot] = jnp.concatenate(
            [jnp.where(low, packed, 0.0), jnp.where(low, pltpu.roll(packed, head_size, 1), 0.0)], axis=0
        ).astype(jnp.bfloat16)

    row_id = lax.broadcasted_iota(jnp.int32, (rows, LANES), 0)
    col_id = lax.broadcasted_iota(jnp.int32, (rows, LANES), 1)

    def visit_tile(slot, block, tile, masked):
        key_value = kv_all[pl.ds(tile * blocks_per_tile, blocks_per_tile)]
        key_value = key_value.reshape(key_tile, LANES)
        scores = lax.dot_general(
            query_buf[slot], key_value, (((1,), (1,)), ((), ())), preferred_element_type=jnp.float32
        )
        query_stamp = stamp_rows[slot]
        weights = []
        for first in range(0, key_tile, LANES):
            elapsed = query_stamp - stamp_keys[tile, :, first : first + LANES]
            bias = jnp.take_along_axis(table, lax.clz(elapsed), axis=1, mode="promise_in_bounds")
            halved = scores[:, first : first + LANES] + bias
            weight = halved + halved * jnp.tanh(halved)
            if masked:
                ahead = tile * key_tile + first - block * rows
                weight = jnp.where(col_id + ahead <= row_id, weight, 0.0)
            weights.append(weight.astype(jnp.bfloat16))
        total_buf[slot] += jnp.dot(
            jnp.concatenate(weights, axis=1), key_value, preferred_element_type=jnp.float32
        )

    def visit_before(slot, group):
        def one(tile, carry):
            visit_tile(slot, 0, tile, False)
            return carry

        lax.fori_loop(group * group_tiles, (group + 1) * group_tiles, one, 0)

    def visit_own(slot):
        block = block_of(slot, my_split)
        last = block // blocks_per_tile

        def one(tile, carry):
            visit_tile(slot, block, tile, False)
            return carry

        if group_tiles > 1:
            lax.fori_loop(slot * group_tiles, last, one, 0)
        visit_tile(slot, block, last, True)

    def send_back(slot, target):
        return remote(
            back_buf.at[slot], att_buf.at[my_head], back_sem.at[slot], att_sem.at[my_head], target
        )

    def finish(slot, carry):
        block = block_of(slot, my_split)
        total = total_buf[slot]
        result = jnp.where(low, pltpu.roll(total[:half], head_size, 1), total[half:]).astype(jnp.bfloat16)
        back_buf[slot] = result

        @pl.when(block == me)
        def _():
            att_buf[my_head] = result

        @pl.when(block != me)
        def _():
            send_back(slot, block).start()

        return carry

    def take_near(slot, carry):
        take_direct(slot)
        take_query(slot)
        return carry

    lax.fori_loop(near_first, near_first + near, take_near, 0)

    def near_group(group, carry):
        take_forwarded(group)
        visit_own(group)

        def one(slot, inner):
            visit_before(slot, group)
            return inner

        lax.fori_loop(group + 1, near_first + near, one, 0)
        return carry

    lax.fori_loop(near_first, near_first + near, near_group, 0)

    lower_end = near * (1 - upper)
    lax.fori_loop(0, lower_end, finish, 0)

    def far_query(slot, carry):
        take_query(slot)
        return carry

    def later_query(step, carry):
        slot = near + step
        take_query(slot)

        def one(group, inner):
            visit_before(slot, group)
            return inner

        lax.fori_loop(0, near, one, 0)
        return carry

    lax.fori_loop(0, lower_end, later_query, 0)
    lax.fori_loop(0, near * upper, far_query, 0)

    def far_at(step):
        return far_first + lax.rem(my_place - step + near, near)

    take_direct(far_at(0))

    def far_group(step, carry):
        group = far_at(step)
        take_forwarded(group)
        visit_own(group)

        def one(slot, inner):
            visit_before(slot, group)
            return inner

        lax.fori_loop(group + 1, slots, one, 0)

        @pl.when(step + 1 < near)
        def _():
            take_direct(far_at(step + 1))

        return carry

    lax.fori_loop(0, near, far_group, 0)
    lax.fori_loop(lower_end, slots, finish, 0)

    def drain_both(head, target):
        q_copy(head, target).wait_send()
        kv_copy(head, target).wait_send()

    each_head(near_first, drain_both)
    each_head(far_first, drain_both)

    def drain(step, carry):
        stamp_copy(lax.rem(me + step, parts)).wait_send()
        return carry

    lax.fori_loop(1, parts, drain, 0)

    def drain_slot(slot, carry):
        source = block_of(slot, my_split)
        for step in range(1, splits):
            forward(slot, source, step).wait_send()

        @pl.when(source != me)
        def _():
            send_back(slot, source).wait_send()

        return carry

    lax.fori_loop(0, slots, drain_slot, 0)
    loads[6].wait()
    loads[7].wait()

    def take_back(step, carry):
        head = lax.rem(my_head + step, heads)
        source = head * splits + my_home

        @pl.when(source != me)
        def _():
            remote(
                back_buf.at[0], att_buf.at[head], back_sem.at[0], att_sem.at[head], source
            ).wait_recv()

        return carry

    lax.fori_loop(0, heads, take_back, 0)

    pieces = []
    for pair in range(heads // 2):
        even = att_buf[2 * pair].astype(jnp.float32)
        odd = att_buf[2 * pair + 1].astype(jnp.float32)
        pieces.append(
            jnp.concatenate(
                [
                    jnp.where(low, even, pltpu.roll(odd, head_size, 1)),
                    jnp.where(low, pltpu.roll(even, head_size, 1), odd),
                ],
                axis=0,
            )
        )
    attended = jnp.concatenate(pieces, axis=1)
    gated = layer_norm(attended, attn_gain_ref[...]) * gate_buf[...].astype(jnp.float32)
    mixed = tokens_ref[...].astype(jnp.float32) + jnp.dot(
        gated.astype(jnp.bfloat16), w_out_ref[...], preferred_element_type=jnp.float32
    )
    out_ref[...] = mixed.astype(jnp.bfloat16)


def solution(mesh):
    parts = mesh.shape["pb"]

    def body(tokens, stamps, norm_gain, w_proj, rel_bias, attn_gain, w_out):
        rows, width = tokens.shape
        heads = rel_bias.shape[0]
        splits = parts // heads
        slots = parts // splits
        blocks_per_tile = max(1, 384 // rows)
        vmem = pl.BlockSpec(memory_space=pltpu.VMEM)
        return pl.pallas_call(
            functools.partial(kernel, parts, heads),
            out_shape=jax.ShapeDtypeStruct((rows, width), jnp.bfloat16),
            in_specs=[pl.BlockSpec(memory_space=pltpu.HBM)] * 7,
            out_specs=vmem,
            scratch_shapes=[
                pltpu.VMEM((rows, width), jnp.bfloat16),
                pltpu.VMEM((1, rows), jnp.int32),
                pltpu.VMEM((1, width), jnp.float32),
                pltpu.VMEM(w_proj.shape, jnp.bfloat16),
                pltpu.SMEM(rel_bias.shape, jnp.float32),
                pltpu.VMEM((1, width), jnp.float32),
                pltpu.VMEM(w_out.shape, jnp.bfloat16),
                pltpu.VMEM((heads, rows, LANES), jnp.bfloat16),
                pltpu.VMEM((heads, rows // 2, LANES), jnp.bfloat16),
                pltpu.VMEM((parts, rows, LANES), jnp.bfloat16),
                pltpu.VMEM((slots, rows // 2, LANES), jnp.bfloat16),
                pltpu.VMEM((slots, rows, LANES), jnp.bfloat16),
                pltpu.VMEM((parts, 1, rows), jnp.int32),
                pltpu.VMEM((parts // blocks_per_tile, 1, blocks_per_tile * rows), jnp.int32),
                pltpu.VMEM((slots, rows, LANES), jnp.int32),
                pltpu.VMEM((slots, rows, LANES), jnp.float32),
                pltpu.VMEM((rows, width), jnp.bfloat16),
                pltpu.VMEM((slots, rows // 2, LANES), jnp.bfloat16),
                pltpu.VMEM((heads, rows // 2, LANES), jnp.bfloat16),
                pltpu.SemaphoreType.DMA((8,)),
                pltpu.SemaphoreType.DMA((heads,)),
                pltpu.SemaphoreType.DMA((heads,)),
                pltpu.SemaphoreType.DMA((slots, splits)),
                pltpu.SemaphoreType.DMA((parts,)),
                pltpu.SemaphoreType.DMA((slots,)),
                pltpu.SemaphoreType.DMA((parts,)),
                pltpu.SemaphoreType.DMA((parts,)),
                pltpu.SemaphoreType.DMA((slots,)),
                pltpu.SemaphoreType.DMA((heads,)),
            ],
            compiler_params=pltpu.CompilerParams(
                collective_id=0, has_side_effects=True
            ),
        )(
            tokens,
            stamps.reshape(1, rows),
            norm_gain.reshape(1, width),
            w_proj,
            rel_bias,
            attn_gain.reshape(1, width),
            w_out,
        )

    return jax.shard_map(
        body,
        mesh=mesh,
        in_specs=(P(("groups", "pb"), None), P(("groups", "pb")), P(), P(), P(), P(), P()),
        out_specs=P(("groups", "pb"), None),
        check_vma=False,
    )
```

time: 47.9 us -> 42.6 us (0.89)
  local copies, waits for them, and re-layouts: 6.96 us -> 1.62 us
    unnamed x15 -> x1, local copies, waits for them, and re-layouts: 6.96 us -> 1.62 us
where the time goes in v2:
time: 42.6 us; the launch traced here: 42.4 us
  Pallas kernels  40.8 us (96%)
  local copies, waits for them, and re-layouts  1.62 us (4%)
    pallas_call x1, Pallas kernels, body(): pl.pallas_call(functools.partial(kernel, parts, heads), out_shape=jax.Sha...  40.8 us
    unnamed x1, local copies, waits for them, and re-layouts  1.62 us

profile of v2, /device:TPU:0, one launch (start us, length us, event | category | flops | bytes accessed | tf_op | source)
XLA Modules:
  0.0 42.4 jit_solution(14152762241995967927)
XLA Ops:
  0.0 40.8 %shard_map.73 = bf16[192,512]{1,0:T(8,128)(2,1)} custom-call(bf16[192,512]{1,0:T(8,128)(2,1)} %tokens_hbm.1, s32[1,192]{1,0:T(1,128)} %bitcast.5, f32[1,512]{1,0:T(1,128)} %bitcast.3, bf16[512,2048]{1,0:T(8,128)(2,1)} %w_proj_hbm.1, f32[8,16]{1,0:T(8,128)} %bias_hbm.1, f32[1,512]{1,0:T(1,128)} %bitcast.4, bf16[512,512]{1,0:T(8,128)(2,1)} %w_out_hbm.1), custom_call_target="tpu_custom_call" | custom-call | tf_op jit(solution)/shard_map/pallas_call | solution.py:473
  40.8 1.6 %copy.9 = bf16[192,512]{1,0:T(8,128)(2,1)} copy(bf16[192,512]{1,0:T(8,128)(2,1)} %shard_map.73) | data formatting | bytes 393216

commit v3 on v2

--- a/solution.py
+++ b/solution.py
@@ -380,22 +380,32 @@
     def far_group(step, carry):
         group = far_at(step)
         take_forwarded(group)
-        visit_own(group)
 
         def one(slot, inner):
             visit_before(slot, group)
             return inner
 
+        @pl.when(step + 1 < near)
+        def _():
+            take_direct(far_at(step + 1))
+
+        visit_own(group)
         lax.fori_loop(group + 1, slots, one, 0)
-
-        @pl.when(step + 1 < near)
-        def _():
-            take_direct(far_at(step + 1))
-
-        return carry
-
-    lax.fori_loop(0, near, far_group, 0)
-    lax.fori_loop(lower_end, slots, finish, 0)
+        return carry
+
+    lax.fori_loop(0, near - 1, far_group, 0)
+
+    last_group = far_at(near - 1)
+    lax.fori_loop(lower_end, last_group, finish, 0)
+    take_forwarded(last_group)
+    visit_own(last_group)
+    finish(last_group, 0)
+
+    def last_one(slot, carry):
+        visit_before(slot, last_group)
+        return finish(slot, carry)
+
+    lax.fori_loop(last_group + 1, slots, last_one, 0)
 
     def drain_both(head, target):
         q_copy(head, target).wait_send()

time: 42.6 us -> 37.7 us (0.88)
  Pallas kernels: 40.8 us -> 35.7 us
    pallas_call x1, Pallas kernels: 40.8 us -> 35.7 us  [body(): pl.pallas_call(functools.partial(kernel, parts, heads), out_shape=jax.Sha...]
where the time goes in v3:
time: 37.7 us; the launch traced here: 37.3 us
  Pallas kernels  35.7 us (95%)
  local copies, waits for them, and re-layouts  1.62 us (4%)
    pallas_call x1, Pallas kernels, body(): pl.pallas_call(functools.partial(kernel, parts, heads), out_shape=jax.Sha...  35.7 us
    unnamed x1, local copies, waits for them, and re-layouts  1.62 us

profile of v3, /device:TPU:0, one launch (start us, length us, event | category | flops | bytes accessed | tf_op | source)
XLA Modules:
  0.0 37.3 jit_solution(5495034695287063584)
XLA Ops:
  0.0 35.7 %shard_map.73 = bf16[192,512]{1,0:T(8,128)(2,1)} custom-call(bf16[192,512]{1,0:T(8,128)(2,1)} %tokens_hbm.1, s32[1,192]{1,0:T(1,128)} %bitcast.5, f32[1,512]{1,0:T(1,128)} %bitcast.3, bf16[512,2048]{1,0:T(8,128)(2,1)} %w_proj_hbm.1, f32[8,16]{1,0:T(8,128)} %bias_hbm.1, f32[1,512]{1,0:T(1,128)} %bitcast.4, bf16[512,512]{1,0:T(8,128)(2,1)} %w_out_hbm.1), custom_call_target="tpu_custom_call" | custom-call | tf_op jit(solution)/shard_map/pallas_call | solution.py:483
  35.7 1.6 %copy.9 = bf16[192,512]{1,0:T(8,128)(2,1)} copy(bf16[192,512]{1,0:T(8,128)(2,1)} %shard_map.73) | data formatting | bytes 393216

commit v4 on v3

--- a/solution.py
+++ b/solution.py
@@ -207,7 +207,8 @@
     table = jnp.zeros((8, LANES), jnp.float32)
     for bucket_id in range(buckets):
         table = jnp.where(bucket == bucket_id, 0.5 * bias_ref[my_head, bucket_id], table)
-    table = jnp.broadcast_to(table[:1], (rows, LANES))
+    table_two = jnp.broadcast_to(table[:1], (2 * rows, LANES))
+    table = table_two[:rows]
 
     def wait_stamps(step, carry):
         source = lax.rem(me + step, parts)
@@ -291,6 +292,42 @@
             jnp.concatenate(weights, axis=1), key_value, preferred_element_type=jnp.float32
         )
 
+    def visit_two(slot, group):
+        def one(tile, carry):
+            key_value = kv_all[pl.ds(tile * blocks_per_tile, blocks_per_tile)]
+            key_value = key_value.reshape(key_tile, LANES)
+            queries = query_buf[pl.ds(slot, 2)].reshape(2 * rows, LANES)
+            query_stamp = stamp_rows[pl.ds(slot, 2)].reshape(2 * rows, LANES)
+            scores = lax.dot_general(
+                queries, key_value, (((1,), (1,)), ((), ())), preferred_element_type=jnp.float32
+            )
+            weights = []
+            for first in range(0, key_tile, LANES):
+                elapsed = query_stamp - stamp_keys[tile, :, first : first + LANES]
+                bias = jnp.take_along_axis(table_two, lax.clz(elapsed), axis=1, mode="promise_in_bounds")
+                halved = scores[:, first : first + LANES] + bias
+                weights.append((halved + halved * jnp.tanh(halved)).astype(jnp.bfloat16))
+            sums = jnp.dot(
+                jnp.concatenate(weights, axis=1), key_value, preferred_element_type=jnp.float32
+            )
+            total_buf[pl.ds(slot, 2)] += sums.reshape(2, rows, LANES)
+            return carry
+
+        lax.fori_loop(group * group_tiles, (group + 1) * group_tiles, one, 0)
+
+    def visit_later(first, end, group):
+        count = end - first
+
+        def two(step, carry):
+            visit_two(first + 2 * step, group)
+            return carry
+
+        lax.fori_loop(0, count // 2, two, 0)
+
+        @pl.when(count % 2 == 1)
+        def _():
+            visit_before(end - 1, group)
+
     def visit_before(slot, group):
         def one(tile, carry):
             visit_tile(slot, 0, tile, False)
@@ -342,11 +379,7 @@
         take_forwarded(group)
         visit_own(group)
 
-        def one(slot, inner):
-            visit_before(slot, group)
-            return inner
-
-        lax.fori_loop(group + 1, near_first + near, one, 0)
+        visit_later(group + 1, near_first + near, group)
         return carry
 
     lax.fori_loop(near_first, near_first + near, near_group, 0)
@@ -358,19 +391,13 @@
         take_query(slot)
         return carry
 
-    def later_query(step, carry):
-        slot = near + step
-        take_query(slot)
-
-        def one(group, inner):
-            visit_before(slot, group)
-            return inner
-
-        lax.fori_loop(0, near, one, 0)
-        return carry
-
-    lax.fori_loop(0, lower_end, later_query, 0)
-    lax.fori_loop(0, near * upper, far_query, 0)
+    lax.fori_loop(far_first, far_first + near, far_query, 0)
+
+    def later_queries(group, carry):
+        visit_later(near, slots, group)
+        return carry
+
+    lax.fori_loop(0, lower_end, later_queries, 0)
 
     def far_at(step):
         return far_first + lax.rem(my_place - step + near, near)
@@ -381,16 +408,12 @@
         group = far_at(step)
         take_forwarded(group)
 
-        def one(slot, inner):
-            visit_before(slot, group)
-            return inner
-
         @pl.when(step + 1 < near)
         def _():
             take_direct(far_at(step + 1))
 
         visit_own(group)
-        lax.fori_loop(group + 1, slots, one, 0)
+        visit_later(group + 1, slots, group)
         return carry
 
     lax.fori_loop(0, near - 1, far_group, 0)

time: 37.7 us -> 35.5 us (0.942)
  Pallas kernels: 35.7 us -> 33.7 us
    pallas_call x1, Pallas kernels: 35.7 us -> 33.7 us  [body(): pl.pallas_call(functools.partial(kernel, parts, heads), out_shape=jax.Sha...]
where the time goes in v4:
time: 35.5 us; the launch traced here: 35.4 us
  Pallas kernels  33.7 us (95%)
  local copies, waits for them, and re-layouts  1.62 us (5%)
    pallas_call x1, Pallas kernels, body(): pl.pallas_call(functools.partial(kernel, parts, heads), out_shape=jax.Sha...  33.7 us
    unnamed x1, local copies, waits for them, and re-layouts  1.62 us

profile of v4, /device:TPU:0, one launch (start us, length us, event | category | flops | bytes accessed | tf_op | source)
XLA Modules:
  0.0 35.4 jit_solution(9146875017477104938)
XLA Ops:
  0.0 33.7 %shard_map.73 = bf16[192,512]{1,0:T(8,128)(2,1)} custom-call(bf16[192,512]{1,0:T(8,128)(2,1)} %tokens_hbm.1, s32[1,192]{1,0:T(1,128)} %bitcast.5, f32[1,512]{1,0:T(1,128)} %bitcast.3, bf16[512,2048]{1,0:T(8,128)(2,1)} %w_proj_hbm.1, f32[8,16]{1,0:T(8,128)} %bias_hbm.1, f32[1,512]{1,0:T(1,128)} %bitcast.4, bf16[512,512]{1,0:T(8,128)(2,1)} %w_out_hbm.1), custom_call_target="tpu_custom_call" | custom-call | tf_op jit(solution)/shard_map/pallas_call | solution.py:506
  33.8 1.6 %copy.9 = bf16[192,512]{1,0:T(8,128)(2,1)} copy(bf16[192,512]{1,0:T(8,128)(2,1)} %shard_map.73) | data formatting | bytes 393216
